TPU v7x, 32 devices: a whole 2x2x4 slice. The times are simulated.
32 devices in a mesh: dp: 4 (over y, core), expert: 4 (over z), tensor: 2 (over x).
Axes of the slice: x: 2, y: 2, z: 4, core: 2. Of those that a mesh axis runs over, the one named last changes fastest.
Arguments:
- router_input: bfloat16 [1024, 2048], P(('dp', 'expert'), 'tensor'), may hold values from -6 to 6
- router_weight: bfloat16 [2048, 8], replicated, may hold values from -0.125 to 0.125
- expert_ids: int32 [1024, 2], P(('dp', 'expert', 'tensor')), may hold values from 0 to 7, all different within a row; in each aligned block of 32 rows (0 to 31, 32 to 63, ...) at most 9 rows name the same one
- down_weight: bfloat16 [61440, 2048], P(('expert', 'tensor')), may hold values from -0.0625 to 0.0625
- hidden: bfloat16 [4, 72, 61440], P('dp', None, ('expert', 'tensor')), may hold values from -6 to 6
- grad_output: bfloat16 [1024, 2048], P(('dp', 'expert', 'tensor')), may hold values from -4 to 4
Outputs:
- weight_grad: bfloat16 [61440, 2048], P(('expert', 'tensor', 'dp'))
- hidden_grad: bfloat16 [4, 72, 61440], P('dp', None, ('expert', 'tensor'))
- router_grad: float32 [2048, 8], replicated
- input_grad: bfloat16 [1024, 2048], P(('dp', 'expert', 'tensor'))
Inputs may be any that keep to these rules, and one draw needn't show every extreme that they name: `expert_ids`: each row names 2 different experts. Within the 32 rows of one device no expert is named more than 9 times, and some device's rows name some expert exactly 9 times.
All inputs are finite; a program needn't handle non-finite values.
Results may differ from a plain program's by a relative error of at most 0.018.
Values may be sent and summed in bfloat16 or wider, within the bound.
No kernel may reach another device: no remote copies, remote signals or barrier semaphores. Data moves between devices by JAX's collectives and lax.ppermute only.
A program may use at most 192 MiB of HBM per device.

v0:
```python
import jax
import jax.numpy as jnp
from jax import lax
from jax.sharding import PartitionSpec as P


def per_device(router_input, router_weight, expert_ids, down_weight, hidden, grad_output):
    token_rows = grad_output.shape[0]
    model_width = grad_output.shape[1]
    expert_count = router_weight.shape[1]
    choose_count = expert_ids.shape[1]
    expert_ranks = lax.axis_size("expert")
    tensor_ranks = lax.axis_size("tensor")
    sources = expert_ranks * tensor_ranks
    spread = sources // expert_count
    capacity = hidden.shape[1] // sources
    full_input = lax.all_to_all(router_input, "tensor", split_axis=0, concat_axis=1, tiled=True)
    logits = jnp.dot(full_input, router_weight, preferred_element_type=jnp.float32)
    labels = jnp.arange(expert_count, dtype=jnp.int32)
    onehot_int = (expert_ids[:, :, None] == labels).astype(jnp.int32)
    onehot = onehot_int.astype(jnp.float32)
    picked = jnp.sum(onehot * logits[:, None, :], axis=2)
    first_gate = jax.nn.sigmoid(picked[:, 0] - picked[:, 1])
    second_gate = jax.nn.sigmoid(picked[:, 1] - picked[:, 0])
    gate_values = jnp.stack([first_gate, second_gate], axis=1)
    gate_low = gate_values.astype(jnp.bfloat16)
    flat_hits = onehot_int.reshape(token_rows * choose_count, expert_count)
    before = jnp.cumsum(flat_hits, axis=0) - flat_hits
    slot_pos = jnp.sum(before * flat_hits, axis=1).reshape(token_rows, choose_count)
    slot_ids = jnp.arange(capacity, dtype=jnp.int32)
    dispatch_table = onehot[:, :, :, None] * (slot_pos[:, :, None, None] == slot_ids).astype(
        jnp.float32
    )
    slot_table = jnp.sum(dispatch_table, axis=1).astype(jnp.bfloat16)
    packed_grad = jnp.einsum(
        "rec,rd->ecd", slot_table, grad_output, preferred_element_type=jnp.float32
    ).astype(jnp.bfloat16)
    packed_gate = jnp.einsum("rkec,rk->ec", dispatch_table, gate_low.astype(jnp.float32)).astype(
        jnp.bfloat16
    )
    send_grad = jnp.repeat(packed_grad, spread, axis=0)
    send_gate = jnp.repeat(packed_gate, spread, axis=0)
    recv_grad, recv_gate = (
        lax.all_to_all(send_grad, ("expert", "tensor"), split_axis=0, concat_axis=0, tiled=True),
        lax.all_to_all(send_gate, ("expert", "tensor"), split_axis=0, concat_axis=0, tiled=True),
    )
    recv_grad = recv_grad.reshape(sources * capacity, model_width)
    recv_gate = recv_gate.reshape(sources * capacity).astype(jnp.float32)
    hidden_rows = hidden[0]
    gated_grad = (recv_gate[:, None] * recv_grad.astype(jnp.float32)).astype(jnp.bfloat16)
    expert_image = lax.dot_general(
        recv_grad, down_weight, (((1,), (1,)), ((), ())), preferred_element_type=jnp.float32
    )
    hidden_part = (recv_gate[:, None] * expert_image).astype(jnp.bfloat16)
    gate_partial = jnp.sum(hidden_rows.astype(jnp.float32) * expert_image, axis=1).reshape(
        sources, capacity
    )
    returned = lax.all_to_all(
        gate_partial, ("expert", "tensor"), split_axis=0, concat_axis=0, tiled=True
    )
    expert_sums = jnp.sum(returned.reshape(expert_count, spread, capacity), axis=1)
    gate_grad = jnp.einsum("rkec,ec->rk", dispatch_table, expert_sums)
    mixed_term = jnp.sum(gate_values * gate_grad, axis=1, keepdims=True)
    logit_part = gate_values * (gate_grad - mixed_term)
    logit_grad = jnp.sum(onehot * logit_part[:, :, None], axis=1)
    input_grad = jnp.dot(
        logit_grad, router_weight.astype(jnp.float32).T, precision=lax.Precision.HIGHEST
    ).astype(jnp.bfloat16)
    router_local = jnp.dot(
        full_input.astype(jnp.float32).T, logit_grad, precision=lax.Precision.HIGHEST
    )
    router_grad = lax.psum(router_local, ("dp", "expert", "tensor"))
    weight_sum = lax.psum_scatter(
        lax.dot_general(
            hidden_rows, gated_grad, (((0,), (0,)), ((), ())), preferred_element_type=jnp.float32
        ).astype(jnp.bfloat16),
        "dp",
        scatter_dimension=0,
        tiled=True,
    )
    return (weight_sum, hidden_part[None], router_grad, input_grad)


def solution(mesh):
    return jax.shard_map(
        per_device,
        mesh=mesh,
        in_specs=(
            P(("dp", "expert"), "tensor"),
            P(),
            P(("dp", "expert", "tensor"), None),
            P(("expert", "tensor"), None),
            P("dp", None, ("expert", "tensor")),
            P(("dp", "expert", "tensor"), None),
        ),
        out_specs=(
            P(("expert", "tensor", "dp"), None),
            P("dp", None, ("expert", "tensor")),
            P(),
            P(("dp", "expert", "tensor"), None),
        ),
        check_vma=False,
    )
```

profile of v0, /device:TPU:0, one launch (start us, length us, event | category | flops | bytes accessed | tf_op | source)
XLA Modules:
  0.0 359.2 jit_solution(10456292851233868904)
XLA Ops:
  8.0 4.4 %all-to-all-start = ((bf16[2,32,1024]{2,1,0:T(8,128)(2,1)}), bf16[2,32,1024]{2,1,0:T(8,128)(2,1)S(1)}, u32[]{:S(2)}, u32[]{:S(2)}) async-start(bf16[2,32,1024]{2,1,0:T(8,128)(2,1)} %bitcast.52), calls=%async_computation | async-start | bytes 262144 | tf_op jit(solution)/shard_map/all_to_all | solution.py:17
  12.4 0.8 copy.28
  13.2 0.7 convert_convert_fusion
  14.5 2.4 all-to-all-done
  17.0 0.9 fusion.15
  17.9 0.7 multiply_reduce_fusion.3
  18.9 0.6 copy.31
  19.5 5.4 %all-to-all-start.1 = ((bf16[8,1,9]{2,1,0:T(2,128)(2,1)}), bf16[8,1,9]{2,1,0:T(2,128)(2,1)S(1)}, u32[]{:S(2)}, u32[]{:S(2)}) async-start(bf16[8,1,9]{2,1,0:T(2,128)(2,1)} %copy.31), calls=%async_computation.1 | async-start | bytes 8192 | tf_op jit(solution)/shard_map/all_to_all | solution.py:45
  24.9 1.1 convolution_convert_fusion
  26.0 5.3 %all-to-all-done.1 = bf16[8,1,9]{2,1,0:T(2,128)(2,1)S(1)} async-done(((bf16[8,1,9]{2,1,0:T(2,128)(2,1)}), bf16[8,1,9]{2,1,0:T(2,128)(2,1)S(1)}, u32[]{:S(2)}, u32[]{:S(2)}) %all-to-all-start.1) | async-done | bytes 176 | tf_op jit(solution)/shard_map/all_to_all | solution.py:45
  31.3 3.5 all-to-all-start.2
  34.9 12.0 %all-to-all-done.2 = bf16[8,9,2048]{2,1,0:T(8,128)(2,1)S(1)} async-done(((bf16[8,9,2048]{2,1,0:T(8,128)(2,1)}), bf16[8,9,2048]{2,1,0:T(8,128)(2,1)S(1)}, u32[]{:S(2)}, u32[]{:S(2)}) %all-to-all-start.2) | async-done | bytes 294944 | tf_op jit(solution)/shard_map/all_to_all | solution.py:44
  47.1 15.5 %multiply_reduce_fusion = (f32[72]{0:T(128)S(1)}, bf16[1,72,7680]{2,1,0:T(8,128)(2,1)}) fusion(bf16[1,72,7680]{2,1,0:T(8,128)(2,1)S(1)} %copy-done.2, f32[72]{0:T(128)S(1)} %reshape.65, bf16[72,2048]{1,0:T(8,128)(2,1)S(1)} %reshape.63, bf16[7680,2048]{1,0:T(8,128)(2,1)} %param.9), kind=kOutput, calls=%fused_computation.4 | convolution fusion | flops 2267688960 | bytes 33964608 | tf_op jit(solution)/shard_map/dot_general | solution.py:51
  62.6 0.7 all_to_all.36
  63.3 3.7 %all-to-all-start.3 = ((f32[8,1,9]{2,1,0:T(1,128)}), f32[8,1,9]{2,1,0:T(1,128)S(1)}, u32[]{:S(2)}, u32[]{:S(2)}) async-start(f32[8,1,9]{2,1,0:T(1,128)} %bitcast.12), calls=%async_computation.3 | async-start | bytes 8192 | tf_op jit(solution)/shard_map/all_to_all | solution.py:58
  67.3 6.1 %all-to-all-done.3 = f32[8,1,9]{2,1,0:T(1,128)S(1)} async-done(((f32[8,1,9]{2,1,0:T(1,128)}), f32[8,1,9]{2,1,0:T(1,128)S(1)}, u32[]{:S(2)}, u32[]{:S(2)}) %all-to-all-start.3) | async-done | bytes 320 | tf_op jit(solution)/shard_map/all_to_all | solution.py:58
  73.6 0.8 convolution_bitcast_fusion
  74.5 13.9 %convert_bitcast_fusion = bf16[7680,2048]{0,1:T(8,128)(2,1)} fusion(bf16[72,2048]{1,0:T(8,128)(2,1)S(1)} %convert_element_type.93, bf16[1,72,7680]{2,1,0:T(8,128)(2,1)S(1)} %copy-done.2), kind=kOutput, calls=%fused_computation | convolution fusion | flops 2280652800 | bytes 32858112 | tf_op jit(solution)/shard_map/dot_general | solution.py:74
  88.4 40.7 %copy.43 = bf16[7680,2048]{1,0:T(8,128)(2,1)} copy(bf16[7680,2048]{0,1:T(8,128)(2,1)} %convert_bitcast_fusion) | data formatting | bytes 62914560
  129.1 0.7 copy-done.3
  129.8 1.0 convolution_convert_fusion.1
  130.8 159.6 %all-reduce.2.cloned.1.call-done = f32[2048,8]{0,1:T(8,128)} async-done(((f32[2048,8]{0,1:T(8,128)}), f32[2048,8]{0,1:T(8,128)}) %all-reduce.2.cloned.1.call-update) | async-done | bytes 65552 | tf_op jit(solution)/shard_map/psum | solution.py:72
  290.4 59.9 %reduce-scatter.4.cloned.1.call-done = bf16[1920,2048]{1,0:T(8,128)(2,1)} async-done(((bf16[7680,2048]{1,0:T(8,128)(2,1)}), bf16[1920,2048]{1,0:T(8,128)(2,1)}) %reduce-scatter.4.cloned.1.call-update) | async-done | bytes 7864336
  350.2 1.5 copy.55
  (37 shorter events, 1.9 us)
Async XLA Ops:
  8.0 16.9 %copy-start = (bf16[32,2048]{1,0:T(8,128)(2,1)S(1)}, bf16[32,2048]{1,0:T(8,128)(2,1)}, u32[]{:S(2)}) copy-start(bf16[32,2048]{1,0:T(8,128)(2,1)} %param.11) | copy-start | bytes 393220
  8.0 39.1 %copy-start.2 = (bf16[1,72,7680]{2,1,0:T(8,128)(2,1)S(1)}, bf16[1,72,7680]{2,1,0:T(8,128)(2,1)}, u32[]{:S(2)}) copy-start(bf16[1,72,7680]{2,1,0:T(8,128)(2,1)} %param.10) | copy-start | bytes 3317764
  8.0 8.9 %all-to-all-start = ((bf16[2,32,1024]{2,1,0:T(8,128)(2,1)}), bf16[2,32,1024]{2,1,0:T(8,128)(2,1)S(1)}, u32[]{:S(2)}, u32[]{:S(2)}) async-start(bf16[2,32,1024]{2,1,0:T(8,128)(2,1)} %bitcast.52), calls=%async_computation | async-start | bytes 262144 | tf_op jit(solution)/shard_map/all_to_all | solution.py:17
  19.5 11.8 %all-to-all-start.1 = ((bf16[8,1,9]{2,1,0:T(2,128)(2,1)}), bf16[8,1,9]{2,1,0:T(2,128)(2,1)S(1)}, u32[]{:S(2)}, u32[]{:S(2)}) async-start(bf16[8,1,9]{2,1,0:T(2,128)(2,1)} %copy.31), calls=%async_computation.1 | async-start | bytes 8192 | tf_op jit(solution)/shard_map/all_to_all | solution.py:45
  31.3 15.6 %all-to-all-start.2 = ((bf16[8,9,2048]{2,1,0:T(8,128)(2,1)}), bf16[8,9,2048]{2,1,0:T(8,128)(2,1)S(1)}, u32[]{:S(2)}, u32[]{:S(2)}) async-start(bf16[8,9,2048]{2,1,0:T(8,128)(2,1)} %convolution_convert_fusion), calls=%async_computation.2 | async-start | bytes 1048576 | tf_op jit(solution)/shard_map/all_to_all | solution.py:44
  47.1 26.5 %copy-start.4 = (s32[32,2]{0,1:T(2,128)S(1)}, s32[32,2]{0,1:T(2,128)}, u32[]{:S(2)}) copy-start(s32[32,2]{0,1:T(2,128)} %param.8) | copy-start | bytes 772
  63.3 10.1 %all-to-all-start.3 = ((f32[8,1,9]{2,1,0:T(1,128)}), f32[8,1,9]{2,1,0:T(1,128)S(1)}, u32[]{:S(2)}, u32[]{:S(2)}) async-start(f32[8,1,9]{2,1,0:T(1,128)} %bitcast.12), calls=%async_computation.3 | async-start | bytes 8192 | tf_op jit(solution)/shard_map/all_to_all | solution.py:58
  67.0 223.4 %all-reduce.2.cloned.1.call-start = ((), (), s32[]{:S(2)}) async-start(), calls=%async_computation.5 | async-start | bytes 131072 | tf_op jit(solution)/shard_map/psum | solution.py:72
  74.5 275.8 %reduce-scatter.4.cloned.1.call-start = ((), (), s32[]{:S(2)}) async-start(), calls=%async_computation.6 | async-start | bytes 39321600
  129.0 0.8 copy-start.3
  129.8 221.9 %copy-start.1 = (bf16[32,2048]{1,0:T(8,128)(2,1)S(1)}, bf16[32,2048]{1,0:T(8,128)(2,1)}, u32[]{:S(2)}) copy-start(bf16[32,2048]{1,0:T(8,128)(2,1)} %param.11) | copy-start | bytes 393220
Sparse Core Ops, SparseCore 0:
  74.6 215.7 all-reduce.1
Sparse Core Ops, SparseCore 1:
  129.2 221.0 reduce-scatter.3
where the time goes:
time: 361 us; the launch traced here: 359 us
  waiting for transfers between devices  245 us (68%)
  local copies, waits for them, and re-layouts  45.8 us (13%)
  matrix products  33.3 us (9%)
  starting transfers between devices  17 us (5%)
  between operations  15.6 us (4%)
    psum x1, waiting for transfers between devices, per_device(): router_grad = lax.psum(router_local, ('dp', 'expert', 'tensor'))  160 us
    unnamed x3, waiting for transfers between devices  59.9 us
    unnamed x14, local copies, waits for them, and re-layouts  43.7 us
    dot_general x1, matrix products, per_device(): lax.dot_general(recv_grad, down_weight, (((1,), (1,)), ((), ())), preferr...  15.5 us
    dot_general x1, matrix products, per_device(): lax.dot_general(hidden_rows, gated_grad, (((0,), (0,)), ((), ())), prefer...  13.9 us
    all_to_all x1, waiting for transfers between devices, per_device(): lax.all_to_all(send_grad, ('expert', 'tensor'), split_axis=0, concat_axis...  12 us
  transfers between devices with their start and end apart: 6, of which 6 were waited for; matrix products, arithmetic and copies ran while one was open for 16% of the time, Pallas kernels for 0%

commit v1 on v0

v1 whole, which is shorter than its diff:
```python
import functools

import jax
import jax.numpy as jnp
from jax import lax
from jax.experimental import pallas as pl
from jax.experimental.pallas import tpu as pltpu
from jax.sharding import PartitionSpec as P


def is_pow2(n):
    return n & (n - 1) == 0


def peer_perm(n, r):
    if is_pow2(n):
        return [(j, j ^ r) for j in range(n)]
    return [(j, (j + r) % n) for j in range(n)]


def peer_target(i, n, r):
    return i ^ r if is_pow2(n) else (i + r) % n


def gather_order(n):
    if not is_pow2(n):
        return list(range(n))
    order, bit = [0], n // 2
    while bit:
        order = order + [r ^ bit for r in order]
        bit //= 2
    return order


def gather_rows(x, axis):
    n = lax.axis_size(axis)
    if not is_pow2(n):
        return jnp.concatenate([x] + [lax.ppermute(x, axis, peer_perm(n, r)) for r in range(1, n)], axis=0)
    bit = n // 2
    while bit:
        far = lax.ppermute(x, axis, peer_perm(n, bit))
        x = jnp.concatenate([x, far], axis=0)
        bit = bit // 2
    return x


def sum_over(x, axis):
    n = lax.axis_size(axis)
    low = x.astype(jnp.bfloat16)
    parts = [lax.ppermute(low, axis, peer_perm(n, r)) for r in range(1, n)]
    total = low.astype(jnp.float32)
    for p in parts:
        total = total + p.astype(jnp.float32)
    return total


def features_of_own_rows(x, axis):
    n = lax.axis_size(axis)
    i = lax.axis_index(axis)
    blocks = x.reshape(n, x.shape[0] // n, x.shape[1])
    take = lambda b: lax.dynamic_index_in_dim(blocks, b, 0, keepdims=False)
    parts = [take(i)] + [
        lax.ppermute(take(peer_target(i, n, r)), axis, peer_perm(n, r)) for r in range(1, n)
    ]
    if n == 1:
        return parts[0]
    if n == 2:
        low = jnp.where(i == 0, parts[0], parts[1])
        high = jnp.where(i == 0, parts[1], parts[0])
        return jnp.concatenate([low, high], axis=1)
    stacked = jnp.stack(parts)
    ordered = [
        lax.dynamic_index_in_dim(stacked, (i ^ h) if is_pow2(n) else (i - h) % n, 0, keepdims=False)
        for h in range(n)
    ]
    return jnp.concatenate(ordered, axis=1)


def image_kernel(steps, rows_step, x_ref, gate_ref, w_hbm, h_hbm, o_hbm, acc_ref, wb, hb, ob, ws, hs, os):
    def w_copy(i):
        return pltpu.make_async_copy(w_hbm.at[pl.ds(i * rows_step, rows_step)], wb.at[i], ws.at[i])

    def h_copy(i):
        return pltpu.make_async_copy(h_hbm.at[:, pl.ds(i * rows_step, rows_step)], hb.at[i], hs.at[i])

    def o_copy(i):
        return pltpu.make_async_copy(ob.at[i], o_hbm.at[:, pl.ds(i * rows_step, rows_step)], os.at[i])

    def begin(i, carry):
        w_copy(i).start()
        h_copy(i).start()
        return carry

    lax.fori_loop(0, steps, begin, 0)
    acc_ref[...] = jnp.zeros_like(acc_ref)

    def step(i, carry):
        w_copy(i).wait()
        h_copy(i).wait()
        image = lax.dot_general(
            wb[i], x_ref[...], (((1,), (1,)), ((), ())), preferred_element_type=jnp.float32
        ).T
        ob[i] = (gate_ref[...] * image).astype(jnp.bfloat16)
        o_copy(i).start()
        prod = hb[i].astype(jnp.float32) * image
        total = prod[:, :128]
        for k in range(1, rows_step // 128):
            total = total + prod[:, k * 128 : (k + 1) * 128]
        acc_ref[...] += total
        return carry

    lax.fori_loop(0, steps, step, 0)

    def finish(i, carry):
        o_copy(i).wait()
        return carry

    lax.fori_loop(0, steps, finish, 0)


def expert_image(recv_grad, recv_gate, down_weight, hidden_rows):
    rows, width = recv_grad.shape
    units = down_weight.shape[0]
    rows_step = max(c for c in range(128, 1281, 128) if units % c == 0)
    steps = units // rows_step
    return pl.pallas_call(
        functools.partial(image_kernel, steps, rows_step),
        in_specs=[
            pl.BlockSpec(memory_space=pltpu.VMEM),
            pl.BlockSpec(memory_space=pltpu.VMEM),
            pl.BlockSpec(memory_space=pl.ANY),
            pl.BlockSpec(memory_space=pl.ANY),
        ],
        out_specs=[pl.BlockSpec(memory_space=pl.ANY), pl.BlockSpec(memory_space=pltpu.VMEM)],
        out_shape=[
            jax.ShapeDtypeStruct((rows, units), jnp.bfloat16),
            jax.ShapeDtypeStruct((rows, 128), jnp.float32),
        ],
        scratch_shapes=[
            pltpu.VMEM((steps, rows_step, width), jnp.bfloat16),
            pltpu.VMEM((steps, rows, rows_step), jnp.bfloat16),
            pltpu.VMEM((steps, rows, rows_step), jnp.bfloat16),
            pltpu.SemaphoreType.DMA((steps,)),
            pltpu.SemaphoreType.DMA((steps,)),
            pltpu.SemaphoreType.DMA((steps,)),
        ],
        compiler_params=pltpu.CompilerParams(vmem_limit_bytes=50 * 2**20),
        cost_estimate=pl.CostEstimate(
            flops=2 * rows * units * width,
            bytes_accessed=2 * units * (width + 2 * rows),
            transcendentals=0,
        ),
        name="expert_image",
    )(recv_grad, recv_gate, down_weight, hidden_rows)


def device_step(router_input, router_weight, expert_ids, down_weight, hidden, grad_output):
    token_rows, model_width = grad_output.shape
    expert_count = router_weight.shape[1]
    choose_count = expert_ids.shape[1]
    ranks = ("expert", "tensor")
    sources = lax.axis_size("expert") * lax.axis_size("tensor")
    spread = sources // expert_count
    groups = lax.axis_size("dp")
    group = lax.axis_index("dp")
    capacity = hidden.shape[1] // sources
    hidden_rows = hidden[0]
    units_own = hidden_rows.shape[1] // groups
    whole_gather = groups * hidden_rows.shape[0] * model_width <= 2**21

    take_units = lambda g: lax.dynamic_slice_in_dim(hidden_rows, g * units_own, units_own, axis=1)
    hidden_parts = [
        lax.ppermute(take_units(peer_target(group, groups, r)), "dp", peer_perm(groups, r)) if r else take_units(group)
        for r in (gather_order(groups) if whole_gather else range(groups))
    ]

    full_input = features_of_own_rows(router_input, "tensor")
    logits = jnp.dot(full_input, router_weight, preferred_element_type=jnp.float32)
    labels = jnp.arange(expert_count, dtype=jnp.int32)
    onehot_int = (expert_ids[:, :, None] == labels).astype(jnp.int32)
    onehot = onehot_int.astype(jnp.float32)
    picked = jnp.sum(onehot * logits[:, None, :], axis=2)
    first_gate = jax.nn.sigmoid(picked[:, 0] - picked[:, 1])
    second_gate = jax.nn.sigmoid(picked[:, 1] - picked[:, 0])
    gate_values = jnp.stack([first_gate, second_gate], axis=1)
    gate_low = gate_values.astype(jnp.bfloat16)

    flat_hits = onehot_int.reshape(token_rows * choose_count, expert_count)
    earlier = jnp.tril(jnp.ones((token_rows * choose_count,) * 2, jnp.bfloat16), -1)
    before = jnp.dot(earlier, flat_hits.astype(jnp.bfloat16), preferred_element_type=jnp.float32)
    slot_pos = jnp.sum(before * flat_hits, axis=1).astype(jnp.int32).reshape(token_rows, choose_count)
    slot_ids = jnp.arange(capacity, dtype=jnp.int32)
    dispatch_table = onehot[:, :, :, None] * (slot_pos[:, :, None, None] == slot_ids).astype(jnp.float32)
    slot_table = jnp.sum(dispatch_table, axis=1).reshape(token_rows, expert_count * capacity)
    packed_grad = lax.dot_general(
        slot_table.astype(jnp.bfloat16), grad_output, (((0,), (0,)), ((), ())),
        preferred_element_type=jnp.float32,
    ).astype(jnp.bfloat16)
    packed_gate = jnp.sum(
        dispatch_table * gate_low.astype(jnp.float32)[:, :, None, None], axis=(0, 1)
    ).astype(jnp.bfloat16)

    lanes = 128
    lines = capacity * model_width // lanes
    gate_lines = -(-capacity // lanes) * 8
    send_grad = packed_grad.reshape(expert_count, lines, lanes)
    send_gate = jnp.pad(packed_gate, ((0, 0), (0, gate_lines * lanes - capacity))).reshape(
        expert_count, gate_lines, lanes
    )
    send = jnp.repeat(jnp.concatenate([send_grad, send_gate], axis=1), spread, axis=0)
    recv = lax.all_to_all(send, ranks, split_axis=0, concat_axis=0, tiled=True)
    recv_grad = recv[:, :lines].reshape(sources * capacity, model_width)
    recv_gate = (
        recv[:, lines:].reshape(sources, gate_lines * lanes)[:, :capacity]
        .reshape(sources * capacity, 1)
        .astype(jnp.float32)
    )
    gated_grad = (recv_gate * recv_grad.astype(jnp.float32)).astype(jnp.bfloat16)
    gated_all = gather_rows(gated_grad, "dp") if whole_gather else None

    hidden_part, partial_lanes = expert_image(recv_grad, recv_gate, down_weight, hidden_rows)
    gate_partial = jnp.sum(partial_lanes, axis=1).reshape(sources, 1, capacity)
    returned = lax.all_to_all(gate_partial, ranks, split_axis=0, concat_axis=0, tiled=True)
    expert_sums = jnp.sum(returned.reshape(expert_count, spread, capacity), axis=1)
    gate_grad = jnp.sum(dispatch_table * expert_sums, axis=(2, 3))
    mixed_term = jnp.sum(gate_values * gate_grad, axis=1, keepdims=True)
    logit_part = gate_values * (gate_grad - mixed_term)
    logit_grad = jnp.sum(onehot * logit_part[:, :, None], axis=1)
    input_grad = jnp.dot(
        logit_grad, router_weight.astype(jnp.float32).T, precision=lax.Precision.HIGHEST
    ).astype(jnp.bfloat16)
    router_part = lax.dot_general(
        logit_grad, full_input.astype(jnp.float32), (((0,), (0,)), ((), ())),
        precision=lax.Precision.HIGHEST,
    )
    for axis in ("tensor", "dp", "expert"):
        router_part = sum_over(router_part, axis)
    rows_dims = (((0,), (0,)), ((), ()))
    if whole_gather:
        hidden_all, gated_all = lax.optimization_barrier((jnp.concatenate(hidden_parts, axis=0), gated_all))
        weight_sum = lax.dot_general(hidden_all, gated_all, rows_dims, preferred_element_type=jnp.float32)
    else:
        weight_sum, gated = 0.0, gated_grad
        for r in range(groups):
            if r:
                gated, _ = lax.optimization_barrier((gated_grad, weight_sum))
                gated = lax.ppermute(gated, "dp", peer_perm(groups, r))
            weight_sum += lax.dot_general(hidden_parts[r], gated, rows_dims, preferred_element_type=jnp.float32)
    weight_sum = weight_sum.astype(jnp.bfloat16)
    return weight_sum, hidden_part[None], router_part.T, input_grad


def solution(mesh):
    return jax.shard_map(
        device_step,
        mesh=mesh,
        in_specs=(
            P(("dp", "expert"), "tensor"),
            P(),
            P(("dp", "expert", "tensor"), None),
            P(("expert", "tensor"), None),
            P("dp", None, ("expert", "tensor")),
            P(("dp", "expert", "tensor"), None),
        ),
        out_specs=(
            P(("expert", "tensor", "dp"), None),
            P("dp", None, ("expert", "tensor")),
            P(),
            P(("dp", "expert", "tensor"), None),
        ),
        check_vma=False,
    )
```

time: 361 us -> 79.5 us (0.22)
  waiting for transfers between devices: 245 us -> 25.9 us
  local copies, waits for them, and re-layouts: 45.8 us -> 3.46 us
  matrix products: 33.3 us -> 8.88 us
  between operations: 15.6 us -> 0.89 us
  Pallas kernels: 0 us -> 13 us
  starting transfers between devices: 17 us -> 22.6 us
    psum x1 -> x0, waiting for transfers between devices: 160 us -> none  [per_device(): router_grad = lax.psum(router_local, ('dp', 'expert', 'tensor'))]
    unnamed x3 -> x0, waiting for transfers between devices: 59.9 us -> none
    unnamed x14 -> x11, local copies, waits for them, and re-layouts: 43.7 us -> 0.8 us
    dot_general x7 -> x6, matrix products: 33.3 us -> 8.88 us  [the longest x1 6.44 us: device_step(): lax.dot_general(hidden_all, gated_all, rows_dims, preferred_element_type=...]
    pallas_call x0 -> x1, Pallas kernels: none -> 13 us  [expert_image(): pl.pallas_call(functools.partial(image_kernel, steps, rows_step), in_spec...]
    ppermute x0 -> x13, waiting for transfers between devices: none -> 12.9 us  [the longest x3 7.55 us: device_step(): lax.ppermute(take_units(peer_target(group, groups, r)), 'dp', peer_perm(g...]
    all_to_all x4 -> x2, waiting for transfers between devices: 25.9 us -> 12.9 us  [the longest x1 8.83 us: device_step(): recv = lax.all_to_all(send, ranks, split_axis=0, concat_axis=0, tiled=True)]
    ppermute x0 -> x13, starting transfers between devices: none -> 12.7 us  [the longest x7 7.07 us: sum_over(): parts = [lax.ppermute(low, axis, peer_perm(n, r)) for r in range(1, n)]]
  transfers between devices with their start and end apart: 6 -> 15, of which waited for: 6 -> 9; matrix products, arithmetic and copies ran while one was open for 16% -> 6% of each run, Pallas kernels for 0% -> 0%
where the time goes in v1:
time: 79.5 us; the launch traced here: 79.1 us
  waiting for transfers between devices  25.9 us (33%)
  starting transfers between devices  22.6 us (28%)
  Pallas kernels  13 us (16%)
  matrix products  8.88 us (11%)
  other arithmetic  4.4 us (6%)
  local copies, waits for them, and re-layouts  3.46 us (4%)
  between operations  0.89 us (1%)
    pallas_call x1, Pallas kernels, expert_image(): pl.pallas_call(functools.partial(image_kernel, steps, rows_step), in_spec...  13 us
    all_to_all x1, waiting for transfers between devices, device_step(): recv = lax.all_to_all(send, ranks, split_axis=0, concat_axis=0, tiled=True)  8.83 us
    ppermute x3, waiting for transfers between devices, device_step(): lax.ppermute(take_units(peer_target(group, groups, r)), 'dp', peer_perm(g...  7.55 us
    ppermute x7, starting transfers between devices, sum_over(): parts = [lax.ppermute(low, axis, peer_perm(n, r)) for r in range(1, n)]  7.07 us
    dot_general x1, matrix products, device_step(): lax.dot_general(hidden_all, gated_all, rows_dims, preferred_element_type=...  6.44 us
    all_to_all x1, starting transfers between devices, device_step(): recv = lax.all_to_all(send, ranks, split_axis=0, concat_axis=0, tiled=True)  6.34 us
    all_to_all x1, waiting for transfers between devices, device_step(): lax.all_to_all(gate_partial, ranks, split_axis=0, concat_axis=0, tiled=True)  4.11 us
    all_to_all x1, starting transfers between devices, device_step(): lax.all_to_all(gate_partial, ranks, split_axis=0, concat_axis=0, tiled=True)  3.57 us
  transfers between devices with their start and end apart: 15, of which 9 were waited for; matrix products, arithmetic and copies ran while one was open for 6% of the time, Pallas kernels for 0%

profile of v1, /device:TPU:0, one launch (start us, length us, event | category | flops | bytes accessed | tf_op | source)
XLA Modules:
  0.0 79.1 jit_solution(5033931469854358725)
XLA Ops:
  0.7 0.9 %dynamic-slice_bitcast_fusion.4 = bf16[32,1024]{1,0:T(8,128)(2,1)S(1)} fusion(bf16[2,32,1024]{2,1,0:T(8,128)(2,1)} %bitcast.38, s32[]{:T(128)S(6)} %select_n.42), kind=kLoop, calls=%fused_computation.27 | loop fusion | bytes 131076 | tf_op jit(solution)/shard_map/jit(dynamic_index_in_dim)/squeeze | solution.py:61
  1.5 3.0 %collective-permute-start.3 = (bf16[32,1024]{1,0:T(8,128)(2,1)S(1)}, bf16[32,1024]{1,0:T(8,128)(2,1)S(1)}, u32[]{:S(2)}, u32[]{:S(2)}) collective-permute-start(bf16[32,1024]{1,0:T(8,128)(2,1)S(1)} %dynamic-slice_bitcast_fusion.4), channel_id=1, source_target_pairs={{0,1},{1,0},{2,3},{3,2},{4,5},{5,4},{6,7},{7,6},{8,9},{9,8},{10,11... | collective-permute-start | bytes 196616 | tf_op jit(solution)/shard_map/ppermute | solution.py:63
  4.5 0.8 copy.25
  5.8 0.7 convert_convert_fusion
  6.7 0.9 %bitcast_select_fusion.1 = (bf16[32,1024]{1,0:T(8,128)(2,1)S(1)}, bf16[32,1024]{1,0:T(8,128)(2,1)S(1)}) fusion(bf16[32,1024]{1,0:T(8,128)(2,1)S(1)} %collective-permute-done.3, pred[]{:T(512)S(6)} %eq.58, bf16[2,32,1024]{2,1,0:T(8,128)(2,1)} %bitcast.39, s32[]{:T(128)S(6)} %select_n.41), kind=kLoop, calls=%fused_computation.23 | loop fusion | flops 65536 | bytes 262149 | tf_op jit(solution)/shard_map/jit(_where)/select_n | solution.py:68
  7.6 0.9 %fusion.1 = f32[32,8]{0,1:T(8,128)S(1)} fusion(bf16[2048,8]{0,1:T(8,128)(2,1)} %param.7, bf16[32,1024]{1,0:T(8,128)(2,1)S(1)} %get-tuple-element.19, bf16[32,1024]{1,0:T(8,128)(2,1)S(1)} %get-tuple-element.18), kind=kOutput, calls=%fused_computation.19 | convolution fusion | flops 1310720 | bytes 164864 | tf_op jit(solution)/shard_map/dot_general | solution.py:178
  8.5 0.7 multiply_reduce_fusion.2
  9.9 0.7 pad_maximum_fusion.3
  10.7 6.3 %all-to-all-start = ((bf16[8,152,128]{2,1,0:T(8,128)(2,1)}), bf16[8,152,128]{2,1,0:T(8,128)(2,1)S(1)}, u32[]{:S(2)}, u32[]{:S(2)}) async-start(bf16[8,152,128]{2,1,0:T(8,128)(2,1)} %pad_maximum_fusion.3), calls=%async_computation | async-start | bytes 622592 | tf_op jit(solution)/shard_map/all_to_all | solution.py:211
  17.0 8.8 %all-to-all-done = bf16[8,152,128]{2,1,0:T(8,128)(2,1)S(1)} async-done(((bf16[8,152,128]{2,1,0:T(8,128)(2,1)}), bf16[8,152,128]{2,1,0:T(8,128)(2,1)S(1)}, u32[]{:S(2)}, u32[]{:S(2)}) %all-to-all-start) | async-done | bytes 311328 | tf_op jit(solution)/shard_map/all_to_all | solution.py:211
  26.1 13.0 %expert_image.1 = (bf16[72,7680]{1,0:T(8,128)(2,1)}, f32[72,128]{1,0:T(8,128)S(1)}) custom-call(bf16[72,2048]{1,0:T(8,128)(2,1)S(1)} %reshape.130.x_ref, f32[72,1]{1,0:T(8,128)S(1)} %reshape.134.gate_ref, bf16[7680,2048]{1,0:T(8,128)(2,1)} %w_hbm.1, bf16[72,7680]{1,0:T(8,128)(2,1)S(1)} %bitcast.36), custom_call_target="tpu_custom_call" | custom-call | flops 2264924160 | bytes 33669120 | tf_op jit(solution)/shard_map/expert_image/pallas_call | solution.py:126
  40.0 3.6 %all-to-all-start.1 = ((f32[8,1,9]{2,1,0:T(1,128)}), f32[8,1,9]{2,1,0:T(1,128)S(1)}, u32[]{:S(2)}, u32[]{:S(2)}) async-start(f32[8,1,9]{2,1,0:T(1,128)} %bitcast.10), calls=%async_computation.1 | async-start | bytes 8192 | tf_op jit(solution)/shard_map/all_to_all | solution.py:223
  43.7 1.6 %collective-permute-start.1 = (bf16[72,1920]{1,0:T(8,128)(2,1)S(1)}, bf16[72,1920]{1,0:T(8,128)(2,1)S(1)}, u32[]{:S(2)}, u32[]{:S(2)}) collective-permute-start(bf16[72,1920]{1,0:T(8,128)(2,1)S(1)} %get-tuple-element.15), channel_id=1, source_target_pairs={{0,8},{8,0},{16,24},{24,16},{1,9},{9,1},{17,25},{25,17},{2,10},{10... | collective-permute-start | bytes 829448 | tf_op jit(solution)/shard_map/ppermute | solution.py:173
  45.8 4.1 %all-to-all-done.1 = f32[8,1,9]{2,1,0:T(1,128)S(1)} async-done(((f32[8,1,9]{2,1,0:T(1,128)}), f32[8,1,9]{2,1,0:T(1,128)S(1)}, u32[]{:S(2)}, u32[]{:S(2)}) %all-to-all-start.1) | async-done | bytes 320 | tf_op jit(solution)/shard_map/all_to_all | solution.py:223
  51.0 1.5 %collective-permute-done.2 = bf16[72,1920]{1,0:T(8,128)(2,1)S(1)} collective-permute-done((bf16[72,1920]{1,0:T(8,128)(2,1)S(1)}, bf16[72,1920]{1,0:T(8,128)(2,1)S(1)}, u32[]{:S(2)}, u32[]{:S(2)}) %collective-permute-start.2) | collective-permute-done | bytes 276512 | tf_op jit(solution)/shard_map/ppermute | solution.py:173
  52.5 6.0 %collective-permute-done = bf16[72,1920]{1,0:T(8,128)(2,1)S(1)} collective-permute-done((bf16[72,1920]{1,0:T(8,128)(2,1)S(1)}, bf16[72,1920]{1,0:T(8,128)(2,1)S(1)}, u32[]{:S(2)}, u32[]{:S(2)}) %collective-permute-start) | collective-permute-done | bytes 276512 | tf_op jit(solution)/shard_map/ppermute | solution.py:173
  58.9 1.6 %collective-permute-start.8 = (bf16[8,2048]{1,0:T(8,128)(2,1)S(1)}, bf16[8,2048]{1,0:T(8,128)(2,1)S(1)}, u32[]{:S(2)}, u32[]{:S(2)}) collective-permute-start(bf16[8,2048]{1,0:T(8,128)(2,1)S(1)} %add_convert_fusion.1), channel_id=1, source_target_pairs={{0,16},{8,24},{16,0},{24,8},{1,17},{9,25},{17,1},{25,9},{2,18},{10... | collective-permute-start | bytes 98312 | tf_op jit(solution)/shard_map/ppermute | solution.py:50
  61.1 1.2 %collective-permute-done.9 = bf16[8,2048]{1,0:T(8,128)(2,1)S(1)} collective-permute-done((bf16[8,2048]{1,0:T(8,128)(2,1)S(1)}, bf16[8,2048]{1,0:T(8,128)(2,1)S(1)}, u32[]{:S(2)}, u32[]{:S(2)}) %collective-permute-start.9) | collective-permute-done | bytes 32800 | tf_op jit(solution)/shard_map/ppermute | solution.py:50
  62.3 0.9 %collective-permute-done.8 = bf16[8,2048]{1,0:T(8,128)(2,1)S(1)} collective-permute-done((bf16[8,2048]{1,0:T(8,128)(2,1)S(1)}, bf16[8,2048]{1,0:T(8,128)(2,1)S(1)}, u32[]{:S(2)}, u32[]{:S(2)}) %collective-permute-start.8) | collective-permute-done | bytes 32800 | tf_op jit(solution)/shard_map/ppermute | solution.py:50
  63.2 3.9 %collective-permute-start.12 = (bf16[8,2048]{1,0:T(8,128)(2,1)S(1)}, bf16[8,2048]{1,0:T(8,128)(2,1)S(1)}, u32[]{:S(2)}, u32[]{:S(2)}) collective-permute-start(bf16[8,2048]{1,0:T(8,128)(2,1)S(1)} %add_convert_fusion), channel_id=1, source_target_pairs={{0,6},{2,4},{4,2},{6,0},{1,7},{3,5},{5,3},{7,1},{8,14},{10,12},{12... | collective-permute-start | bytes 98312 | tf_op jit(solution)/shard_map/ppermute | solution.py:50
  67.7 2.3 %collective-permute-done.4 = bf16[72,2048]{1,0:T(8,128)(2,1)S(1)} collective-permute-done((bf16[72,2048]{1,0:T(8,128)(2,1)S(1)}, bf16[72,2048]{1,0:T(8,128)(2,1)S(1)}, u32[]{:S(2)}, u32[]{:S(2)}) %collective-permute-start.4) | collective-permute-done | bytes 294944 | tf_op jit(solution)/shard_map/ppermute | solution.py:41
  70.2 1.0 %convolution_convert_fusion.2 = bf16[32,2048]{1,0:T(8,128)(2,1)} fusion(f32[32,8]{0,1:T(8,128)S(1)} %multiply_reduce_fusion.1, bf16[2048,8]{0,1:T(8,128)(2,1)S(1)} %copy-done.2), kind=kOutput, calls=%fused_computation.2 | convolution fusion | flops 6356992 | bytes 164864 | tf_op jit(solution)/shard_map/dot_general | solution.py:229
  71.2 0.7 collective-permute-done.11
  72.6 6.4 %convolution_convert_fusion = bf16[1920,2048]{1,0:T(8,128)(2,1)} fusion(bf16[288,1920]{1,0:T(8,128)(2,1)S(1)} %pad_maximum_fusion.1, bf16[288,2048]{1,0:T(8,128)(2,1)S(1)} %pad_maximum_fusion), kind=kOutput, calls=%fused_computation | convolution fusion | flops 2268856320 | bytes 10149888 | tf_op jit(solution)/shard_map/dot_general | solution.py:241
  (63 shorter events, 6.7 us)
Async XLA Ops:
  0.6 8.9 %copy-start = (bf16[32,2048]{1,0:T(8,128)(2,1)S(1)}, bf16[32,2048]{1,0:T(8,128)(2,1)}, u32[]{:S(2)}) copy-start(bf16[32,2048]{1,0:T(8,128)(2,1)} %param.11) | copy-start | bytes 393220
  1.5 5.2 %collective-permute-start.3 = (bf16[32,1024]{1,0:T(8,128)(2,1)S(1)}, bf16[32,1024]{1,0:T(8,128)(2,1)S(1)}, u32[]{:S(2)}, u32[]{:S(2)}) collective-permute-start(bf16[32,1024]{1,0:T(8,128)(2,1)S(1)} %dynamic-slice_bitcast_fusion.4), channel_id=1, source_target_pairs={{0,1},{1,0},{2,3},{3,2},{4,5},{5,4},{6,7},{7,6},{8,9},{9,8},{10,11... | collective-permute-start | bytes 196616 | tf_op jit(solution)/shard_map/ppermute | solution.py:63
  9.9 16.2 %copy-start.1 = (bf16[1,72,7680]{2,1,0:T(8,128)(2,1)S(1)}, bf16[1,72,7680]{2,1,0:T(8,128)(2,1)}, u32[]{:S(2)}) copy-start(bf16[1,72,7680]{2,1,0:T(8,128)(2,1)} %param.10) | copy-start | bytes 3317764
  10.7 15.2 %all-to-all-start = ((bf16[8,152,128]{2,1,0:T(8,128)(2,1)}), bf16[8,152,128]{2,1,0:T(8,128)(2,1)S(1)}, u32[]{:S(2)}, u32[]{:S(2)}) async-start(bf16[8,152,128]{2,1,0:T(8,128)(2,1)} %pad_maximum_fusion.3), calls=%async_computation | async-start | bytes 622592 | tf_op jit(solution)/shard_map/all_to_all | solution.py:211
  39.1 11.0 %copy-start.3 = (s32[32,2]{0,1:T(2,128)S(1)}, s32[32,2]{0,1:T(2,128)}, u32[]{:S(2)}) copy-start(s32[32,2]{0,1:T(2,128)} %param.8) | copy-start | bytes 772
  40.0 10.0 %all-to-all-start.1 = ((f32[8,1,9]{2,1,0:T(1,128)}), f32[8,1,9]{2,1,0:T(1,128)S(1)}, u32[]{:S(2)}, u32[]{:S(2)}) async-start(f32[8,1,9]{2,1,0:T(1,128)} %bitcast.10), calls=%async_computation.1 | async-start | bytes 8192 | tf_op jit(solution)/shard_map/all_to_all | solution.py:223
  43.6 8.9 %collective-permute-start.2 = (bf16[72,1920]{1,0:T(8,128)(2,1)S(1)}, bf16[72,1920]{1,0:T(8,128)(2,1)S(1)}, u32[]{:S(2)}, u32[]{:S(2)}) collective-permute-start(bf16[72,1920]{1,0:T(8,128)(2,1)S(1)} %get-tuple-element.17), channel_id=1, source_target_pairs={{0,24},{8,16},{16,8},{24,0},{1,25},{9,17},{17,9},{25,1},{2,26},{10... | collective-permute-start | bytes 829448 | tf_op jit(solution)/shard_map/ppermute | solution.py:173
  43.7 8.8 %collective-permute-start.1 = (bf16[72,1920]{1,0:T(8,128)(2,1)S(1)}, bf16[72,1920]{1,0:T(8,128)(2,1)S(1)}, u32[]{:S(2)}, u32[]{:S(2)}) collective-permute-start(bf16[72,1920]{1,0:T(8,128)(2,1)S(1)} %get-tuple-element.15), channel_id=1, source_target_pairs={{0,8},{8,0},{16,24},{24,16},{1,9},{9,1},{17,25},{25,17},{2,10},{10... | collective-permute-start | bytes 829448 | tf_op jit(solution)/shard_map/ppermute | solution.py:173
  45.3 13.2 %collective-permute-start = (bf16[72,1920]{1,0:T(8,128)(2,1)S(1)}, bf16[72,1920]{1,0:T(8,128)(2,1)S(1)}, u32[]{:S(2)}, u32[]{:S(2)}) collective-permute-start(bf16[72,1920]{1,0:T(8,128)(2,1)S(1)} %get-tuple-element.16), channel_id=1, source_target_pairs={{0,16},{8,24},{16,0},{24,8},{1,17},{9,25},{17,1},{25,9},{2,18},{10... | collective-permute-start | bytes 829448 | tf_op jit(solution)/shard_map/ppermute | solution.py:173
  50.4 8.3 %collective-permute-start.6 = (bf16[8,2048]{1,0:T(8,128)(2,1)S(1)}, bf16[8,2048]{1,0:T(8,128)(2,1)S(1)}, u32[]{:S(2)}, u32[]{:S(2)}) collective-permute-start(bf16[8,2048]{1,0:T(8,128)(2,1)S(1)} %convolution_convert_fusion.3), channel_id=1, source_target_pairs={{0,1},{1,0},{2,3},{3,2},{4,5},{5,4},{6,7},{7,6},{8,9},{9,8},{10,11... | collective-permute-start | bytes 98312 | tf_op jit(solution)/shard_map/ppermute | solution.py:50
  58.6 11.6 %copy-start.2 = (bf16[2048,8]{0,1:T(8,128)(2,1)S(1)}, bf16[2048,8]{0,1:T(8,128)(2,1)}, u32[]{:S(2)}) copy-start(bf16[2048,8]{0,1:T(8,128)(2,1)} %param.7) | copy-start | bytes 98308
  58.7 3.5 %collective-permute-start.9 = (bf16[8,2048]{1,0:T(8,128)(2,1)S(1)}, bf16[8,2048]{1,0:T(8,128)(2,1)S(1)}, u32[]{:S(2)}, u32[]{:S(2)}) collective-permute-start(bf16[8,2048]{1,0:T(8,128)(2,1)S(1)} %add_convert_fusion.1), channel_id=1, source_target_pairs={{0,24},{8,16},{16,8},{24,0},{1,25},{9,17},{17,9},{25,1},{2,26},{10... | collective-permute-start | bytes 98312 | tf_op jit(solution)/shard_map/ppermute | solution.py:50
  58.9 4.3 %collective-permute-start.8 = (bf16[8,2048]{1,0:T(8,128)(2,1)S(1)}, bf16[8,2048]{1,0:T(8,128)(2,1)S(1)}, u32[]{:S(2)}, u32[]{:S(2)}) collective-permute-start(bf16[8,2048]{1,0:T(8,128)(2,1)S(1)} %add_convert_fusion.1), channel_id=1, source_target_pairs={{0,16},{8,24},{16,0},{24,8},{1,17},{9,25},{17,1},{25,9},{2,18},{10... | collective-permute-start | bytes 98312 | tf_op jit(solution)/shard_map/ppermute | solution.py:50
  60.4 2.7 %collective-permute-start.7 = (bf16[8,2048]{1,0:T(8,128)(2,1)S(1)}, bf16[8,2048]{1,0:T(8,128)(2,1)S(1)}, u32[]{:S(2)}, u32[]{:S(2)}) collective-permute-start(bf16[8,2048]{1,0:T(8,128)(2,1)S(1)} %add_convert_fusion.1), channel_id=1, source_target_pairs={{0,8},{8,0},{16,24},{24,16},{1,9},{9,1},{17,25},{25,17},{2,10},{10... | collective-permute-start | bytes 98312 | tf_op jit(solution)/shard_map/ppermute | solution.py:50
  60.8 9.3 %collective-permute-start.4 = (bf16[72,2048]{1,0:T(8,128)(2,1)S(1)}, bf16[72,2048]{1,0:T(8,128)(2,1)S(1)}, u32[]{:S(2)}, u32[]{:S(2)}) collective-permute-start(bf16[72,2048]{1,0:T(8,128)(2,1)S(1)} %multiply_convert_fusion), channel_id=1, source_target_pairs={{0,16},{8,24},{16,0},{24,8},{1,17},{9,25},{17,1},{25,9},{2,18},{10... | collective-permute-start | bytes 884744 | tf_op jit(solution)/shard_map/ppermute | solution.py:41
  63.2 8.0 %collective-permute-start.12 = (bf16[8,2048]{1,0:T(8,128)(2,1)S(1)}, bf16[8,2048]{1,0:T(8,128)(2,1)S(1)}, u32[]{:S(2)}, u32[]{:S(2)}) collective-permute-start(bf16[8,2048]{1,0:T(8,128)(2,1)S(1)} %add_convert_fusion), channel_id=1, source_target_pairs={{0,6},{2,4},{4,2},{6,0},{1,7},{3,5},{5,3},{7,1},{8,14},{10,12},{12... | collective-permute-start | bytes 98312 | tf_op jit(solution)/shard_map/ppermute | solution.py:50
  67.1 4.8 %collective-permute-start.11 = (bf16[8,2048]{1,0:T(8,128)(2,1)S(1)}, bf16[8,2048]{1,0:T(8,128)(2,1)S(1)}, u32[]{:S(2)}, u32[]{:S(2)}) collective-permute-start(bf16[8,2048]{1,0:T(8,128)(2,1)S(1)} %add_convert_fusion), channel_id=1, source_target_pairs={{0,4},{2,6},{4,0},{6,2},{1,5},{3,7},{5,1},{7,3},{8,12},{10,14},{12... | collective-permute-start | bytes 98312 | tf_op jit(solution)/shard_map/ppermute | solution.py:50
  67.1 4.8 %collective-permute-start.10 = (bf16[8,2048]{1,0:T(8,128)(2,1)S(1)}, bf16[8,2048]{1,0:T(8,128)(2,1)S(1)}, u32[]{:S(2)}, u32[]{:S(2)}) collective-permute-start(bf16[8,2048]{1,0:T(8,128)(2,1)S(1)} %add_convert_fusion), channel_id=1, source_target_pairs={{0,2},{2,0},{4,6},{6,4},{1,3},{3,1},{5,7},{7,5},{8,10},{10,8},{12,... | collective-permute-start | bytes 98312 | tf_op jit(solution)/shard_map/ppermute | solution.py:50
  70.1 2.5 %collective-permute-start.5 = (bf16[144,2048]{1,0:T(8,128)(2,1)S(1)}, bf16[144,2048]{1,0:T(8,128)(2,1)S(1)}, u32[]{:S(2)}, u32[]{:S(2)}) collective-permute-start(bf16[144,2048]{1,0:T(8,128)(2,1)S(1)} %pad_maximum_fusion.2), channel_id=1, source_target_pairs={{0,8},{8,0},{16,24},{24,16},{1,9},{9,1},{17,25},{25,17},{2,10},{10... | collective-permute-start | bytes 1769480 | tf_op jit(solution)/shard_map/ppermute | solution.py:41
